TPU v7x, 256 devices: a whole 4x4x8 slice. The times are simulated.
256 devices in a mesh: expert: 16 (over y, x), wide: 16 (over z, core).
Axes of the slice: x: 4, y: 4, z: 8, core: 2. Of those that a mesh axis runs over, the one named last changes fastest.
Arguments:
- tokens: bfloat16 [32768, 2048], P(('expert', 'wide')), may hold values from -6 to 6
- out_grad: bfloat16 [32768, 2048], P(('expert', 'wide')), may hold values from -6 to 6
- routes: int32 [32768, 2], P(('expert', 'wide')), may hold values from 0 to 15, all different within a row; in each aligned block of 128 rows (0 to 127, 128 to 255, ...) at most 32 rows name the same one
- gate_prob: float32 [32768, 2], P(('expert', 'wide')), may hold values from 0.1 to 1
- w_gate: bfloat16 [16, 2048, 768], P('expert', 'wide'), may hold values from -0.125 to 0.125
- w_up: bfloat16 [16, 2048, 768], P('expert', 'wide'), may hold values from -0.125 to 0.125
- w_down: bfloat16 [16, 2048, 768], P('expert', 'wide'), may hold values from -0.21875 to 0.21875
Outputs:
- grad_input: bfloat16 [32768, 2048], P(('expert', 'wide'))
- grad_gate: float32 [16, 2048, 768], P('expert', 'wide')
- grad_up: float32 [16, 2048, 768], P('expert', 'wide')
- grad_down: float32 [16, 2048, 768], P('expert', 'wide')
Inputs may be any that keep to these rules, and one draw needn't show every extreme that they name: `routes`: each row names 2 different experts; the 128 rows of one device name one expert at most 32 times, and in every draw some device names some expert exactly 32 times.
All inputs are finite; a program needn't handle non-finite values.
Results may differ from a plain program's by a relative error of at most 0.017.
Values may be sent and summed in bfloat16 or wider, within the bound.
A program may use at most 128 MiB of HBM per device.

v0:
```python
import jax
import jax.numpy as jnp
from jax import lax
from jax.sharding import PartitionSpec as P


def swish_backward(gate_pre, up_pre, hidden_grad):
    squash = jax.nn.sigmoid(gate_pre)
    active = gate_pre * squash
    hidden = (active * up_pre).astype(jnp.bfloat16)
    gate_act = (hidden_grad * up_pre * squash * (1.0 + gate_pre * (1.0 - squash))).astype(
        jnp.bfloat16
    )
    up_act = (hidden_grad * active).astype(jnp.bfloat16)
    return (hidden, gate_act, up_act)


def on_device(tokens, out_grad, routes, gate_prob, w_gate, w_up, w_down):
    experts = lax.axis_size("expert")
    tok_count = routes.shape[0]
    top_count = routes.shape[1]
    capacity = min(tok_count, 2 * tok_count * top_count // experts)
    slot_count = experts * capacity
    model_width = tokens.shape[1]
    hidden_units = w_gate.shape[2]
    flat_routes = routes.reshape(-1)
    one_hot = (flat_routes[:, None] == jnp.arange(experts, dtype=jnp.int32)[None, :]).astype(
        jnp.int32
    )
    before = jnp.cumsum(one_hot, axis=0) - one_hot
    positions = flat_routes * capacity + jnp.sum(before * one_hot, axis=1)
    chosen = (positions[None, :] == jnp.arange(slot_count, dtype=jnp.int32)[:, None]).reshape(
        slot_count, tok_count, top_count
    )
    picker = jnp.sum(chosen.astype(jnp.float32), axis=2)
    slot_gate = jnp.sum(jnp.where(chosen, gate_prob[None, :, :], 0.0), axis=(1, 2))
    picker_half = picker.astype(jnp.bfloat16)
    sent_rows = jnp.dot(picker_half, tokens, preferred_element_type=jnp.float32).astype(
        jnp.bfloat16
    )
    sent_grad = (
        jnp.dot(picker_half, out_grad, preferred_element_type=jnp.float32) * slot_gate[:, None]
    ).astype(jnp.bfloat16)
    got_rows, got_grad = (
        lax.all_to_all(
            sent_rows.reshape(experts, capacity, model_width),
            "expert",
            split_axis=0,
            concat_axis=0,
            tiled=True,
        ),
        lax.all_to_all(
            sent_grad.reshape(experts, capacity, model_width),
            "expert",
            split_axis=0,
            concat_axis=0,
            tiled=True,
        ),
    )
    rows_in = got_rows.reshape(slot_count, model_width)
    grad_in = got_grad.reshape(slot_count, model_width)
    pieces = (
        lax.all_gather(w_gate, "wide", axis=1, tiled=True),
        lax.all_gather(w_up, "wide", axis=1, tiled=True),
        lax.all_gather(w_down, "wide", axis=1, tiled=True),
    )
    rows_part = rows_in
    grad_part = grad_in
    gate_pre = jnp.dot(rows_part, pieces[0][0], preferred_element_type=jnp.float32)
    up_pre = jnp.dot(rows_part, pieces[1][0], preferred_element_type=jnp.float32)
    hidden_grad = jnp.dot(grad_part, pieces[2][0], preferred_element_type=jnp.float32)
    hidden, gate_act, up_act = swish_backward(gate_pre, up_pre, hidden_grad)
    merged = jnp.concatenate((gate_act, up_act), axis=1)
    pieces = lax.all_gather((w_gate, w_up), "wide", axis=1, tiled=True)
    stacked = jnp.concatenate((pieces[0][0], pieces[1][0]), axis=1)
    input_grad = lax.dot_general(
        merged, stacked, (((1,), (1,)), ((), ())), preferred_element_type=jnp.float32
    )
    rows_part = rows_in
    grad_part = grad_in
    left_part = lax.dot_general(
        rows_part, merged, (((0,), (0,)), ((), ())), preferred_element_type=jnp.float32
    )
    right_part = lax.dot_general(
        grad_part, hidden, (((0,), (0,)), ((), ())), preferred_element_type=jnp.float32
    )
    summed = lax.psum_scatter(
        jnp.concatenate((left_part, right_part), axis=1).astype(jnp.bfloat16),
        "wide",
        scatter_dimension=0,
        tiled=True,
    ).astype(jnp.float32)
    grad_gate = summed[:, :hidden_units][None]
    grad_up = summed[:, hidden_units : 2 * hidden_units][None]
    grad_down = summed[:, 2 * hidden_units :][None]
    returned = lax.all_to_all(
        input_grad.astype(jnp.bfloat16).reshape(experts, capacity, model_width),
        "expert",
        split_axis=0,
        concat_axis=0,
        tiled=True,
    )
    grad_input = lax.dot_general(
        picker_half,
        returned.reshape(slot_count, model_width),
        (((0,), (0,)), ((), ())),
        preferred_element_type=jnp.float32,
    ).astype(jnp.bfloat16)
    return (grad_input, grad_gate, grad_up, grad_down)


def solution(mesh):
    placed = (
        P(("expert", "wide"), None),
        P(("expert", "wide"), None),
        P(("expert", "wide"), None),
        P(("expert", "wide"), None),
        P("expert", "wide", None),
        P("expert", "wide", None),
        P("expert", "wide", None),
    )
    return jax.shard_map(
        on_device,
        mesh=mesh,
        in_specs=placed,
        out_specs=(
            P(("expert", "wide"), None),
            P("expert", "wide", None),
            P("expert", "wide", None),
            P("expert", "wide", None),
        ),
        check_vma=False,
    )
```

profile of v0, /device:TPU:17, one launch (start us, length us, event | category | flops | bytes accessed | tf_op | source)
XLA Modules:
  0.0 253.0 jit_solution(3616024606060035480)
XLA Ops:
  7.2 0.0 copy-start
  7.2 0.0 all-gather.4.cloned.1.call-start
  7.2 0.7 all-gather.4.cloned.1.call-update
  7.9 0.0 all-gather.6.cloned.1.call-start
  8.0 0.7 all-gather.6.cloned.1.call-update
  8.7 0.0 all-gather.8.cloned.1.call-start
  8.7 0.7 all-gather.8.cloned.1.call-update
  9.4 0.8 copy.43
  10.2 0.1 eq.43
  10.3 0.1 eq.39
  10.5 0.6 reduce-window.6
  11.1 0.2 slice_reduce_fusion
  11.3 0.1 fusion.13
  11.4 0.1 reduce_sum.30
  11.5 0.1 copy.46
  11.6 0.7 multiply_add_fusion
  12.3 0.8 convert_reduce_fusion
  13.2 0.0 copy-done
  13.2 2.1 multiply_convert_fusion
  15.2 6.9 %all-to-all-start = ((bf16[16,32,2048]{2,1,0:T(8,128)(2,1)}), bf16[16,32,2048]{2,1,0:T(8,128)(2,1)S(1)}, u32[]{:S(2)}, u32[]{:S(2)}) async-start(bf16[16,32,2048]{2,1,0:T(8,128)(2,1)} %bitcast.1), calls=%async_computation | async-start | bytes 4194304 | tf_op jit(solution)/shard_map/all_to_all | solution.py:52
  22.1 0.0 copy-done.1
  22.1 2.1 convolution_convert_fusion.2
  24.1 26.6 %all-to-all-done = bf16[16,32,2048]{2,1,0:T(8,128)(2,1)S(1)} async-done(((bf16[16,32,2048]{2,1,0:T(8,128)(2,1)}), bf16[16,32,2048]{2,1,0:T(8,128)(2,1)S(1)}, u32[]{:S(2)}, u32[]{:S(2)}) %all-to-all-start) | async-done | bytes 2097184 | tf_op jit(solution)/shard_map/all_to_all | solution.py:52
  50.7 6.6 %all-to-all-start.1 = ((bf16[16,32,2048]{2,1,0:T(8,128)(2,1)}), bf16[16,32,2048]{2,1,0:T(8,128)(2,1)}, u32[]{:S(2)}, u32[]{:S(2)}) async-start(bf16[16,32,2048]{2,1,0:T(8,128)(2,1)} %bitcast.4), calls=%async_computation.1 | async-start | bytes 4194304 | tf_op jit(solution)/shard_map/all_to_all | solution.py:45
  57.3 0.0 reduce-scatter.4.cloned.1.call-start
  57.4 0.0 all-gather.4.cloned.1.call-done
  57.4 4.9 %fusion.4 = f32[512,768]{1,0:T(8,128)} fusion(bf16[512,2048]{1,0:T(8,128)(2,1)S(1)} %bitcast.55, bf16[1,2048,768]{2,1,0:T(8,128)(2,1)} %all-gather.4.cloned.1.call-done), kind=kOutput, calls=%fused_computation.8 | convolution fusion | flops 1610612736 | bytes 6815744 | tf_op jit(solution)/shard_map/dot_general | solution.py:71
  62.3 21.1 %all-to-all-done.1 = bf16[16,32,2048]{2,1,0:T(8,128)(2,1)} async-done(((bf16[16,32,2048]{2,1,0:T(8,128)(2,1)}), bf16[16,32,2048]{2,1,0:T(8,128)(2,1)}, u32[]{:S(2)}, u32[]{:S(2)}) %all-to-all-start.1) | async-done | bytes 2097184 | tf_op jit(solution)/shard_map/all_to_all | solution.py:45
  83.4 11.2 %all-gather.6.cloned.1.call-done = bf16[1,2048,768]{2,1,0:T(8,128)(2,1)} async-done(((bf16[1,128,768]{2,1,0:T(8,128)(2,1)}), bf16[1,2048,768]{2,1,0:T(8,128)(2,1)}) %all-gather.6.cloned.1.call-update) | async-done | bytes 3145744 | tf_op jit(solution)/shard_map/all_gather | solution.py:64
  94.6 5.5 %fusion.19 = f32[512,768]{1,0:T(8,128)} fusion(bf16[512,2048]{1,0:T(8,128)(2,1)} %bitcast.5, bf16[1,2048,768]{2,1,0:T(8,128)(2,1)} %all-gather.6.cloned.1.call-done), kind=kOutput, calls=%fused_computation.39 | convolution fusion | flops 1610612736 | bytes 6815744 | tf_op jit(solution)/shard_map/dot_general | solution.py:70
  100.1 35.6 %all-gather.8.cloned.1.call-done = bf16[1,2048,768]{2,1,0:T(8,128)(2,1)} async-done(((bf16[1,128,768]{2,1,0:T(8,128)(2,1)}), bf16[1,2048,768]{2,1,0:T(8,128)(2,1)}) %all-gather.8.cloned.1.call-update) | async-done | bytes 3145744 | tf_op jit(solution)/shard_map/all_gather | solution.py:63
  135.7 5.8 %multiply_convert_fusion.3 = (bf16[512,768]{1,0:T(8,128)(2,1)S(1)}, bf16[512,768]{1,0:T(8,128)(2,1)S(1)}, f32[512,768]{1,0:T(8,128)S(1)}) fusion(f32[512,768]{1,0:T(8,128)} %fusion.4, f32[512,768]{1,0:T(8,128)} %fusion.19, bf16[512,2048]{1,0:T(8,128)(2,1)} %bitcast.5, bf16[1,2048,768]{2,1,0:T(8,128)(2,1)} %all-gather.8.cloned.1.call-done), kind=kOutput, calls=%fused_computation.16 | convolution fusion | flops 1615724544 | bytes 11534336 | tf_op jit(solution)/shard_map/dot_general | solution.py:69
  141.5 1.9 convolution_convert_fusion.1
  143.4 5.5 %convolution_convert_fusion = bf16[2048,1536]{0,1:T(8,128)(2,1)S(1)} fusion(bf16[512,2048]{1,0:T(8,128)(2,1)} %bitcast.5, bf16[512,768]{1,0:T(8,128)(2,1)S(1)} %get-tuple-element.27, bf16[512,768]{1,0:T(8,128)(2,1)S(1)} %get-tuple-element.26), kind=kOutput, calls=%fused_computation.1 | convolution fusion | flops 3227516928 | bytes 9961472 | tf_op jit(solution)/shard_map/dot_general | solution.py:81
  148.9 11.3 %pad_maximum_fusion = bf16[2048,2304]{0,1:T(8,128)(2,1)} fusion(bf16[2048,768]{0,1:T(8,128)(2,1)S(1)} %convolution_convert_fusion.1, bf16[2048,1536]{0,1:T(8,128)(2,1)S(1)} %convolution_convert_fusion), kind=kLoop, calls=%fused_computation | loop fusion | flops 18874368 | bytes 18874368 | tf_op jit(solution)/shard_map/concatenate | solution.py:88
  160.3 12.8 %copy.50 = bf16[2048,2304]{1,0:T(8,128)(2,1)} copy(bf16[2048,2304]{0,1:T(8,128)(2,1)} %pad_maximum_fusion) | data formatting | bytes 18874368
  173.1 0.0 reduce-scatter.4.cloned.1.call-update
  173.1 1.1 copy-done.4
  174.2 6.3 %fusion.6 = bf16[512,2048]{1,0:T(8,128)(2,1)S(1)} fusion(bf16[2048,768]{1,0:T(8,128)(2,1)} %bitcast.58, bf16[2048,768]{1,0:T(8,128)(2,1)} %bitcast.59, bf16[512,768]{1,0:T(8,128)(2,1)S(1)} %copy-done.4, bf16[512,768]{1,0:T(8,128)(2,1)S(1)} %get-tuple-element.26), kind=kOutput, calls=%fused_computation.11 | convolution fusion | flops 3238002688 | bytes 9961472 | tf_op jit(solution)/shard_map/dot_general | solution.py:76
  180.5 32.1 %all_to_all.15 = bf16[16,32,2048]{2,1,0:T(8,128)(2,1)S(1)} all-to-all(bf16[16,32,2048]{2,1,0:T(8,128)(2,1)S(1)} %bitcast.57), channel_id=1, replica_groups=mesh['expert'=16,'wide'=16] {'expert'}, dimensions={0} | all-to-all | bytes 4194304 | tf_op jit(solution)/shard_map/all_to_all | solution.py:96
  212.6 1.3 convolution_convert_fusion.3
  213.8 28.3 %reduce-scatter.4.cloned.1.call-done = bf16[128,2304]{1,0:T(8,128)(2,1)} async-done(((bf16[2048,2304]{1,0:T(8,128)(2,1)}), bf16[128,2304]{1,0:T(8,128)(2,1)}) %reduce-scatter.4.cloned.1.call-update) | async-done | bytes 589840
  242.2 1.4 copy.51
  243.5 0.1 convert_element_type.49
  243.6 0.1 slice_bitcast_fusion
  243.7 0.9 copy.49
  244.6 0.9 copy.48
  245.5 0.9 copy.47
  (9 shorter events, 0.1 us)
Async XLA Ops:
  7.2 6.0 %copy-start = (bf16[128,2048]{1,0:T(8,128)(2,1)S(1)}, bf16[128,2048]{1,0:T(8,128)(2,1)}, u32[]{:S(2)}) copy-start(bf16[128,2048]{1,0:T(8,128)(2,1)} %param.8) | copy-start | bytes 1572868
  7.2 50.2 %all-gather.4.cloned.1.call-start = ((), (), s32[]{:S(2)}) async-start(), calls=%async_computation.4 | async-start | bytes 3342336 | tf_op jit(solution)/shard_map/all_gather | solution.py:65
  7.9 86.7 %all-gather.6.cloned.1.call-start = ((), (), s32[]{:S(2)}) async-start(), calls=%async_computation.5 | async-start | bytes 3342336 | tf_op jit(solution)/shard_map/all_gather | solution.py:64
  8.7 127.0 %all-gather.8.cloned.1.call-start = ((), (), s32[]{:S(2)}) async-start(), calls=%async_computation.6 | async-start | bytes 3342336 | tf_op jit(solution)/shard_map/all_gather | solution.py:63
  15.2 6.9 %copy-start.1 = (bf16[128,2048]{1,0:T(8,128)(2,1)S(1)}, bf16[128,2048]{1,0:T(8,128)(2,1)}, u32[]{:S(2)}) copy-start(bf16[128,2048]{1,0:T(8,128)(2,1)} %param.7) | copy-start | bytes 1572868
  15.2 35.5 %all-to-all-start = ((bf16[16,32,2048]{2,1,0:T(8,128)(2,1)}), bf16[16,32,2048]{2,1,0:T(8,128)(2,1)S(1)}, u32[]{:S(2)}, u32[]{:S(2)}) async-start(bf16[16,32,2048]{2,1,0:T(8,128)(2,1)} %bitcast.1), calls=%async_computation | async-start | bytes 4194304 | tf_op jit(solution)/shard_map/all_to_all | solution.py:52
  50.7 32.7 %all-to-all-start.1 = ((bf16[16,32,2048]{2,1,0:T(8,128)(2,1)}), bf16[16,32,2048]{2,1,0:T(8,128)(2,1)}, u32[]{:S(2)}, u32[]{:S(2)}) async-start(bf16[16,32,2048]{2,1,0:T(8,128)(2,1)} %bitcast.4), calls=%async_computation.1 | async-start | bytes 4194304 | tf_op jit(solution)/shard_map/all_to_all | solution.py:45
  57.3 184.8 %reduce-scatter.4.cloned.1.call-start = ((), (), s32[]{:S(2)}) async-start(), calls=%async_computation.7 | async-start | bytes 10027008
  135.7 5.8 %copy-start.2 = (f32[512,768]{1,0:T(8,128)S(1)}, f32[512,768]{1,0:T(8,128)}, u32[]{:S(2)}) copy-start(f32[512,768]{1,0:T(8,128)} %fusion.19) | copy-start | bytes 4718596
  141.5 1.9 copy-start.3
  173.1 1.1 copy-start.4
Sparse Core Ops, SparseCore 0:
  9.8 43.8 all-gather.3
  55.6 38.9 all-gather.5
  96.4 39.2 all-gather.7
  173.2 68.8 reduce-scatter.3
where the time goes:
time: 256 us; the launch traced here: 253 us
  waiting for transfers between devices  125 us (49%)
  matrix products  35.3 us (14%)
  blocking collectives  32.1 us (13%)
  local copies, waits for them, and re-layouts  19.6 us (8%)
  between operations  13.9 us (5%)
  other arithmetic  13.7 us (5%)
  starting transfers between devices  13.6 us (5%)
    all_gather x1, waiting for transfers between devices, on_device(): lax.all_gather(w_gate, 'wide', axis=1, tiled=True)  35.6 us
    all_to_all x1, blocking collectives, on_device(): lax.all_to_all(input_grad.astype(jnp.bfloat16).reshape(experts, capacity,...  32.1 us
    unnamed x5, waiting for transfers between devices  30.4 us
    all_to_all x1, waiting for transfers between devices, on_device(): lax.all_to_all(sent_grad.reshape(experts, capacity, model_width), 'expert...  26.6 us
    all_to_all x1, waiting for transfers between devices, on_device(): lax.all_to_all(sent_rows.reshape(experts, capacity, model_width), 'expert...  21.1 us
    unnamed x16, local copies, waits for them, and re-layouts  18.8 us
    concatenate x1, other arithmetic, on_device(): jnp.concatenate((left_part, right_part), axis=1).astype(jnp.bfloat16)  11.3 us
    all_gather x1, waiting for transfers between devices, on_device(): lax.all_gather(w_up, 'wide', axis=1, tiled=True)  11.2 us
  transfers between devices with their start and end apart: 6, of which 5 were waited for; matrix products, arithmetic and copies ran while one was open for 10% of the time, Pallas kernels for 0%

commit v1 on v0

v1 whole, which is shorter than its diff:
```python
import functools

import jax
import jax.numpy as jnp
from jax import lax
from jax.experimental import pallas as pl
from jax.experimental.pallas import tpu as pltpu
from jax.sharding import PartitionSpec as P

MESH = pl.DeviceIdType.MESH
BF16 = jnp.bfloat16
F32 = jnp.float32
SIDE = 4
EXPERTS = 16
RING = 8
TOK = 128
CAP = 32
ROWS = EXPERTS * CAP
D = 2048
F = 768
HALF = F // 2
BLK = 128
TRIP = 3 * HALF

OFFSETS = sorted(
    [(dy, dx) for dy in range(SIDE) for dx in range(SIDE) if (dy, dx) != (0, 0)],
    key=lambda o: -(min(o[0], SIDE - o[0]) + min(o[1], SIDE - o[1])),
)


def contract(a, b, da, db):
    return lax.dot_general(a, b, (((da,), (db,)), ((), ())), preferred_element_type=F32)


def kernel(
    tok_ref, og_ref, rt_ref, gp_ref, wg_ref, wu_ref, wd_ref,
    gi_ref, gg_ref, gu_ref, gd_ref,
    send_x, send_g, x_ref, g_ref, w_ref, w_other, pt_ref,
    pre_ref, hg_ref, act_ref, hid_ref,
    rs_send, rs_recv, fin_send, fin_recv, own_ref,
    ig_send, ig_recv, ig_own, rg_ref, ret_ref,
    xs_sem, xr_sem, gs_sem, gr_sem, xfs_sem, xfr_sem, gfs_sem, gfr_sem,
    wo_sem, ag_ssem, ag_rsem, rs_ssem, rs_rsem, fin_sem, ig_sem, ret_ssem, ret_rsem,
):
    e = lax.axis_index("expert")
    w = lax.axis_index("wide")
    ey, ex = e // SIDE, lax.rem(e, SIDE)
    z, c = w // 2, lax.rem(w, 2)
    other = 1 - c
    partner = (e, z * 2 + other)

    def zdev(step):
        return (e, lax.rem(z + step + RING, RING) * 2 + c)

    def edev(dy, dx):
        return lax.rem(ey + dy + SIDE, SIDE) * SIDE + lax.rem(ex + dx + SIDE, SIDE)

    def remote(src, dst, ssem, rsem, dev):
        return pltpu.make_async_remote_copy(
            src_ref=src, dst_ref=dst, send_sem=ssem, recv_sem=rsem,
            device_id=dev, device_id_type=MESH,
        )

    def feat(blk):
        return pl.ds(pl.multiple_of(blk * BLK, BLK), BLK)

    def erow(core, ei):
        return pl.ds(pl.multiple_of(core * ROWS + ei * CAP, CAP), CAP)

    barrier = pltpu.get_barrier_semaphore()
    peers = [(edev(dy, dx), w) for dy, dx in OFFSETS] + [zdev(1), zdev(-1), partner]
    for dev in peers:
        pl.semaphore_signal(barrier, inc=1, device_id=dev, device_id_type=MESH)

    mine = pl.ds(pl.multiple_of(c * HALF, BLK), HALF)
    theirs = pl.ds(pl.multiple_of(other * HALF, BLK), HALF)
    for i, ref in enumerate((wg_ref, wu_ref, wd_ref)):
        w_ref[feat(w), i * HALF:(i + 1) * HALF] = ref[:, mine]
        w_other[:, i * HALF:(i + 1) * HALF] = ref[:, theirs]

    routes = rt_ref[...]
    lane = lax.broadcasted_iota(jnp.int32, (TOK, BLK), 1)
    row = lax.broadcasted_iota(jnp.int32, (TOK, BLK), 0)
    hot = [routes[:, k:k + 1] == lane for k in range(2)]
    named = jnp.where(jnp.logical_or(hot[0], hot[1]), 1.0, 0.0).astype(BF16)
    earlier = jnp.where(lane < row, 1.0, 0.0).astype(BF16)
    before = contract(earlier, named, 1, 0)
    slot_lane = lax.broadcasted_iota(jnp.int32, (TOK, ROWS), 1).astype(F32)
    picks = []
    for k in range(2):
        slot = jnp.sum(jnp.where(hot[k], before, 0.0), axis=1, keepdims=True)
        pos = routes[:, k:k + 1].astype(F32) * float(CAP) + slot
        picks.append(jnp.where(pos == slot_lane, 1.0, 0.0))
    pt_ref[...] = (picks[0] + picks[1]).astype(BF16)
    pick = jnp.transpose(picks[0] + picks[1]).astype(BF16)
    for j in range(4):
        cols = slice(j * 512, (j + 1) * 512)
        send_x[:, cols] = contract(pick, tok_ref[:, cols], 1, 0).astype(BF16)

    pl.semaphore_wait(barrier, len(peers))

    swap = remote(w_other, w_ref.at[feat(w)], wo_sem.at[0], wo_sem.at[1], partner)
    swap.start()

    def ag_block(direction, k):
        parity = c if (k % 2 == 0) else other
        if k == 6 and direction < 0:
            parity = other
        blk = lax.rem(z - direction * (k // 2) + 2 * RING, RING)
        return blk * 2 + parity

    def ag_copy(direction, k):
        d = 0 if direction > 0 else 1
        blk = ag_block(direction, k)
        return remote(
            w_ref.at[feat(blk)], w_ref.at[feat(blk)],
            ag_ssem.at[d, k], ag_rsem.at[d, k], zdev(direction),
        )

    ag_copy(1, 0).start()
    ag_copy(-1, 0).start()

    def row_copies(src, dst, ssem, rsem):
        out = []
        for i, (dy, dx) in enumerate(OFFSETS):
            dest = edev(dy, dx)
            out.append(remote(
                src.at[pl.ds(pl.multiple_of(dest * CAP, CAP), CAP)],
                dst.at[erow(c, e)], ssem.at[i], rsem.at[i], (dest, w),
            ))
        return out

    x_sends = row_copies(send_x, x_ref, xs_sem, xr_sem)
    for copy in x_sends:
        copy.start()
    swap.wait()
    ag_copy(1, 1).start()
    ag_copy(-1, 1).start()

    pick_two = jnp.concatenate([jnp.transpose(p).astype(BF16) for p in picks], axis=1)
    gates = [gp_ref[:, k:k + 1] for k in range(2)]
    for j in range(4):
        cols = slice(j * 512, (j + 1) * 512)
        part = og_ref[:, cols].astype(F32)
        both = jnp.concatenate([(part * gates[k]).astype(BF16) for k in range(2)], axis=0)
        send_g[:, cols] = contract(pick_two, both, 1, 0).astype(BF16)
    g_sends = row_copies(send_g, g_ref, gs_sem, gr_sem)
    for copy in g_sends:
        copy.start()

    own_rows = pl.ds(pl.multiple_of(e * CAP, CAP), CAP)
    x_ref[erow(c, e), :] = send_x[own_rows, :]
    g_ref[erow(c, e), :] = send_g[own_rows, :]

    def forward(buf, ssem, rsem, i, src):
        return remote(buf.at[erow(c, src)], buf.at[erow(c, src)], ssem.at[i], rsem.at[i], partner)

    for k in range(7):
        for direction in (1, -1):
            ag_copy(direction, k).wait_recv()
            nxt = k + 2
            if direction < 0 and k == 5:
                ag_copy(direction, 6).start()
            elif nxt <= 6 and not (direction < 0 and k == 4):
                ag_copy(direction, nxt).start()
        if k == 1:
            forward(x_ref, xfs_sem, xfr_sem, 15, e).start()
            forward(g_ref, gfs_sem, gfr_sem, 15, e).start()

    def pass_on(buf, sends, ssem, rsem):
        for i, (dy, dx) in enumerate(OFFSETS):
            sends[i].wait_recv()
            forward(buf, ssem, rsem, i, edev(-dy, -dx)).start()

    def arrived(buf, ssem, rsem):
        for i, (dy, dx) in enumerate(OFFSETS + [(0, 0)]):
            forward(buf, ssem, rsem, i, edev(-dy, -dx)).wait_recv()

    pass_on(x_ref, x_sends, xfs_sem, xfr_sem)
    arrived(x_ref, xfs_sem, xfr_sem)

    def first(t, carry):
        rows = pl.ds(pl.multiple_of((t // 3) * 512, 512), 512)
        cols = pl.ds(pl.multiple_of(lax.rem(t, 3) * 256, 256), 256)
        pre_ref[rows, cols] = contract(x_ref[rows, :], w_ref[:, cols], 1, 0)
        return carry

    lax.fori_loop(0, 6, first, 0)

    pass_on(g_ref, g_sends, gfs_sem, gfr_sem)
    arrived(g_ref, gfs_sem, gfr_sem)

    def second(t, carry):
        rows = pl.ds(pl.multiple_of(t * 512, 512), 512)
        hg_ref[rows, :] = contract(g_ref[rows, :], w_ref[:, 2 * HALF:], 1, 0)
        return carry

    lax.fori_loop(0, 2, second, 0)

    def swish(t, carry):
        rows = pl.ds(pl.multiple_of(t * 32, 32), 32)
        gate_pre = pre_ref[rows, :HALF]
        up_pre = pre_ref[rows, HALF:]
        hidden_grad = hg_ref[rows, :]
        squash = jax.nn.sigmoid(gate_pre)
        active = gate_pre * squash
        hid_ref[rows, :] = (active * up_pre).astype(BF16)
        act_ref[rows, :HALF] = (
            hidden_grad * up_pre * squash * (1.0 + gate_pre * (1.0 - squash))
        ).astype(BF16)
        act_ref[rows, HALF:] = (hidden_grad * active).astype(BF16)
        return carry

    lax.fori_loop(0, 2 * ROWS // 32, swish, 0)

    def rs_chunk(direction, k):
        dist = 4 - (k + 1) // 2
        even = lax.rem(k, 2) == 0
        if direction > 0:
            parity = jnp.where(even, c, other)
        else:
            parity = jnp.where(even, other, c)
        return lax.rem(z + direction * dist + RING, RING) * 2 + parity

    def partial(blk):
        cols = feat(blk)
        left = contract(x_ref[:, cols], act_ref[...], 0, 0)
        right = contract(g_ref[:, cols], hid_ref[...], 0, 0)
        return left, right

    def rs_copy(direction, k):
        d = 0 if direction > 0 else 1
        return remote(
            rs_send.at[d, k], rs_recv.at[d, k], rs_ssem.at[d, k], rs_rsem.at[d, k],
            zdev(direction),
        )

    def rs_step(k, add):
        for direction in (1, -1):
            d = 0 if direction > 0 else 1
            left, right = partial(rs_chunk(direction, k))
            if add:
                rs_copy(direction, k - 2).wait_recv()
                left = left + rs_recv[d, k - 2, :, :2 * HALF].astype(F32)
                right = right + rs_recv[d, k - 2, :, 2 * HALF:].astype(F32)
            rs_send[d, k, :, :2 * HALF] = left.astype(BF16)
            rs_send[d, k, :, 2 * HALF:] = right.astype(BF16)
            rs_copy(direction, k).start()

    def rs_first(k, carry):
        rs_step(k, False)
        return carry

    lax.fori_loop(0, 2, rs_first, 0)

    def input_part(core, j):
        rows = pl.ds(pl.multiple_of(core * ROWS, ROWS), ROWS)
        cols = pl.ds(pl.multiple_of(j * 256, 256), 256)
        return contract(act_ref[rows, :], w_ref[cols, :2 * HALF], 1, 1), cols

    def for_other(j, carry):
        got, cols = input_part(other, j)
        ig_send[:, cols] = got.astype(BF16)
        return carry

    lax.fori_loop(0, 8, for_other, 0)
    ig_copy = remote(ig_send, ig_recv, ig_sem.at[0], ig_sem.at[1], partner)
    ig_copy.start()

    def for_mine(j, carry):
        got, cols = input_part(c, j)
        ig_own[:, cols] = got
        return carry

    lax.fori_loop(0, 8, for_mine, 0)
    ig_copy.wait_recv()

    def join(t, carry):
        rows = pl.ds(pl.multiple_of(t * CAP, CAP), CAP)
        rg_ref[rows, :] = (ig_own[rows, :] + ig_recv[rows, :].astype(F32)).astype(BF16)
        return carry

    lax.fori_loop(0, EXPERTS, join, 0)
    returns = []
    for i, (dy, dx) in enumerate(OFFSETS):
        dest = edev(dy, dx)
        returns.append(remote(
            rg_ref.at[pl.ds(pl.multiple_of(dest * CAP, CAP), CAP)],
            ret_ref.at[own_rows], ret_ssem.at[i], ret_rsem.at[i], (dest, w),
        ))
    for copy in returns:
        copy.start()
    ret_ref[own_rows, :] = rg_ref[own_rows, :]

    def rs_next(k, carry):
        rs_step(k, True)
        return carry

    lax.fori_loop(2, 7, rs_next, 0)

    def keep(p, blk):
        left, right = partial(blk)
        own_ref[p, :, :2 * HALF] = left
        own_ref[p, :, 2 * HALF:] = right

    keep(0, z * 2 + c)
    keep(1, z * 2 + other)

    for copy in returns:
        copy.wait_recv()
    for j in range(4):
        cols = slice(j * 512, (j + 1) * 512)
        gi_ref[:, cols] = contract(pt_ref[...], ret_ref[:, cols], 1, 0).astype(BF16)

    rs_copy(1, 5).wait_recv()
    rs_copy(-1, 5).wait_recv()
    rs_copy(-1, 6).wait_recv()
    fin_send[...] = (
        own_ref[1] + rs_recv[0, 5].astype(F32) + rs_recv[1, 6].astype(F32)
    ).astype(BF16)
    fin = remote(fin_send, fin_recv, fin_sem.at[0], fin_sem.at[1], partner)
    fin.start()
    rs_copy(1, 6).wait_recv()
    mine_sum = own_ref[0] + rs_recv[0, 6].astype(F32) + rs_recv[1, 5].astype(F32)
    for i, ref in enumerate((gg_ref, gu_ref, gd_ref)):
        ref[:, mine] = mine_sum[:, i * HALF:(i + 1) * HALF]
    fin.wait_recv()
    for i, ref in enumerate((gg_ref, gu_ref, gd_ref)):
        ref[:, theirs] = fin_recv[:, i * HALF:(i + 1) * HALF].astype(F32)

    for copy in x_sends + g_sends + returns:
        copy.wait_send()
    for i, (dy, dx) in enumerate(OFFSETS + [(0, 0)]):
        src = edev(-dy, -dx)
        forward(x_ref, xfs_sem, xfr_sem, i, src).wait_send()
        forward(g_ref, gfs_sem, gfr_sem, i, src).wait_send()
    for direction in (1, -1):
        for k in range(7):
            ag_copy(direction, k).wait_send()
            rs_copy(direction, k).wait_send()
    ig_copy.wait_send()
    fin.wait_send()


def on_device(tokens, out_grad, routes, gate_prob, w_gate, w_up, w_down):
    flat = [a.reshape(BLK, F) for a in (w_gate, w_up, w_down)]
    dma = pltpu.SemaphoreType.DMA
    vmem = pl.BlockSpec(memory_space=pltpu.VMEM)
    outs = pl.pallas_call(
        kernel,
        name="moe_back",
        out_shape=(
            jax.ShapeDtypeStruct((TOK, D), BF16),
            jax.ShapeDtypeStruct((BLK, F), F32),
            jax.ShapeDtypeStruct((BLK, F), F32),
            jax.ShapeDtypeStruct((BLK, F), F32),
        ),
        in_specs=[vmem] * 7,
        out_specs=(vmem,) * 4,
        scratch_shapes=[
            pltpu.VMEM((ROWS, D), BF16),
            pltpu.VMEM((ROWS, D), BF16),
            pltpu.VMEM((2 * ROWS, D), BF16),
            pltpu.VMEM((2 * ROWS, D), BF16),
            pltpu.VMEM((D, TRIP), BF16),
            pltpu.VMEM((BLK, TRIP), BF16),
            pltpu.VMEM((TOK, ROWS), BF16),
            pltpu.VMEM((2 * ROWS, F), F32),
            pltpu.VMEM((2 * ROWS, HALF), F32),
            pltpu.VMEM((2 * ROWS, F), BF16),
            pltpu.VMEM((2 * ROWS, HALF), BF16),
            pltpu.VMEM((2, 7, BLK, TRIP), BF16),
            pltpu.VMEM((2, 7, BLK, TRIP), BF16),
            pltpu.VMEM((BLK, TRIP), BF16),
            pltpu.VMEM((BLK, TRIP), BF16),
            pltpu.VMEM((2, BLK, TRIP), F32),
            pltpu.VMEM((ROWS, D), BF16),
            pltpu.VMEM((ROWS, D), BF16),
            pltpu.VMEM((ROWS, D), F32),
            pltpu.VMEM((ROWS, D), BF16),
            pltpu.VMEM((ROWS, D), BF16),
            dma((15,)), dma((15,)), dma((15,)), dma((15,)),
            dma((16,)), dma((16,)), dma((16,)), dma((16,)),
            dma((2,)), dma((2, 7)), dma((2, 7)), dma((2, 7)), dma((2, 7)),
            dma((2,)), dma((2,)), dma((15,)), dma((15,)),
        ],
        compiler_params=pltpu.CompilerParams(
            collective_id=0, has_side_effects=True, vmem_limit_bytes=67043328,
        ),
    )(tokens, out_grad, routes, gate_prob, *flat)
    return (outs[0],) + tuple(o[None] for o in outs[1:])


def solution(mesh):
    rows = P(("expert", "wide"), None)
    weight = P("expert", "wide", None)
    return jax.shard_map(
        on_device,
        mesh=mesh,
        in_specs=(rows,) * 4 + (weight,) * 3,
        out_specs=(rows,) + (weight,) * 3,
        check_vma=False,
    )
```

time: 256 us -> 132 us (0.52)
  the two profiles are of different devices: /device:TPU:17 before, /device:TPU:33 now
where the time goes in v1:
time: 132 us; the launch traced here: 131 us
  Pallas kernels  124 us (94%)
  local copies, waits for them, and re-layouts  7.11 us (5%)
    pallas_call x1, Pallas kernels, on_device(): pl.pallas_call(kernel, name='moe_back', out_shape=(jax.ShapeDtypeStruct((...  124 us
    unnamed x16, local copies, waits for them, and re-layouts  7.11 us

profile of v1, /device:TPU:33, one launch (start us, length us, event | category | flops | bytes accessed | tf_op | source)
XLA Modules:
  0.0 131.3 jit_solution(1212761903791579592)
XLA Ops:
  0.6 0.0 copy-start.3
  0.6 0.7 copy-done.3
  1.3 0.0 copy-start.4
  1.3 0.7 copy.11.rt_ref
  2.1 0.0 copy-done.4
  2.1 0.7 copy.12.gp_ref
  2.8 123.5 %moe_back.1 = (bf16[128,2048]{1,0:T(8,128)(2,1)}, f32[128,768]{1,0:T(8,128)}, f32[128,768]{1,0:T(8,128)}, f32[128,768]{1,0:T(8,128)}) custom-call(bf16[128,2048]{1,0:T(8,128)(2,1)} %tok_ref.1, bf16[128,2048]{1,0:T(8,128)(2,1)} %og_ref.1, s32[128,2]{1,0:T(8,128)} %copy.11.rt_ref, f32[128,2]{1,0:T(8,128)} %copy.12.gp_ref, bf16[128,768]{1,0:T(8,128)(2,1)} %bitcast.9, ...), custom_call_target="tpu_custom_call" | custom-call | tf_op jit(solution)/shard_map/moe_back/pallas_call | solution.py:349
  126.3 0.0 copy-start.2
  126.3 1.9 %copy.17 = bf16[128,2048]{1,0:T(8,128)(2,1)} copy(bf16[128,2048]{1,0:T(8,128)(2,1)} %get-tuple-element.16) | data formatting | bytes 1048576
  128.3 0.0 copy-done.2
  128.3 0.0 copy-start.1
  128.3 0.7 copy.18
  129.0 0.4 copy-done.1
  129.4 0.0 copy-start
  129.4 0.7 copy.19
  130.2 0.4 copy-done
  130.6 0.7 copy.20
Async XLA Ops:
  0.6 0.7 copy-start.3
  1.3 0.7 copy-start.4
  126.3 1.9 %copy-start.2 = (f32[128,768]{1,0:T(8,128)S(1)}, f32[128,768]{1,0:T(8,128)}, u32[]{:S(2)}) copy-start(f32[128,768]{1,0:T(8,128)} %get-tuple-element.9) | copy-start | bytes 1179652
  128.3 1.1 copy-start.1
  129.4 1.1 copy-start

commit v2 on v1

v2 whole, which is shorter than its diff:
```python
import functools

import jax
import jax.numpy as jnp
from jax import lax
from jax.experimental import pallas as pl
from jax.experimental.pallas import tpu as pltpu
from jax.sharding import PartitionSpec as P

MESH = pl.DeviceIdType.MESH
BF16 = jnp.bfloat16
F32 = jnp.float32
SIDE = 4
EXPERTS = 16
RING = 8
TOK = 128
CAP = 32
ROWS = EXPERTS * CAP
D = 2048
F = 768
HALF = F // 2
BLK = 128
TRIP = 3 * HALF

OFFSETS = sorted(
    [(dy, dx) for dy in range(SIDE) for dx in range(SIDE) if (dy, dx) != (0, 0)],
    key=lambda o: -(min(o[0], SIDE - o[0]) + min(o[1], SIDE - o[1])),
)


def contract(a, b, da, db):
    return lax.dot_general(a, b, (((da,), (db,)), ((), ())), preferred_element_type=F32)


def kernel(
    tok_hbm, og_hbm, rt_hbm, gp_hbm, wg_hbm, wu_hbm, wd_hbm,
    gi_ref, gg_ref, gu_ref, gd_ref,
    tok_ref, og_ref, rt_ref, gp_ref,
    send_x, send_g, x_ref, g_ref, wgu_ref, wd_ref, wgu_other, wd_other, pick_ref,
    pre_ref, hg_ref, act_ref, hid_ref,
    sd_send, sd_recv, su_send, su_recv, fin_send, fin_recv, own_ref,
    ig_send, ig_recv, ig_own, rg_ref, ret_ref,
    in_sem, xs_sem, xr_sem, gs_sem, gr_sem, xfs_sem, xfr_sem, gfs_sem, gfr_sem,
    wo_ssem, wo_rsem, ag_ssem, ag_rsem, rs_ssem, rs_rsem, fin_sem, ig_sem, ret_ssem, ret_rsem,
):
    e = lax.axis_index("expert")
    w = lax.axis_index("wide")
    ey, ex = e // SIDE, lax.rem(e, SIDE)
    z, c = w // 2, lax.rem(w, 2)
    other = 1 - c
    partner = (e, z * 2 + other)

    def zdev(step, core):
        return (e, lax.rem(z + step + RING, RING) * 2 + core)

    def edev(dy, dx):
        return lax.rem(ey + dy + SIDE, SIDE) * SIDE + lax.rem(ex + dx + SIDE, SIDE)

    def remote(src, dst, ssem, rsem, dev):
        return pltpu.make_async_remote_copy(
            src_ref=src, dst_ref=dst, send_sem=ssem, recv_sem=rsem,
            device_id=dev, device_id_type=MESH,
        )

    def feat(blk):
        return pl.ds(pl.multiple_of(blk * BLK, BLK), BLK)

    def erow(core, ei):
        return pl.ds(pl.multiple_of(core * ROWS + ei * CAP, CAP), CAP)

    barrier = pltpu.get_barrier_semaphore()
    peers = [(edev(dy, dx), w) for dy, dx in OFFSETS] + [partner]
    peers += [zdev(s, core) for s in (1, -1) for core in (c, other)]
    for dev in peers:
        pl.semaphore_signal(barrier, inc=1, device_id=dev, device_id_type=MESH)

    mine = pl.ds(pl.multiple_of(c * HALF, BLK), HALF)
    theirs = pl.ds(pl.multiple_of(other * HALF, BLK), HALF)
    places = [
        (rt_hbm, rt_ref), (gp_hbm, gp_ref), (tok_hbm, tok_ref),
        (wg_hbm.at[:, mine], wgu_ref.at[feat(w), pl.ds(0, HALF)]),
        (wu_hbm.at[:, mine], wgu_ref.at[feat(w), pl.ds(HALF, HALF)]),
        (wg_hbm.at[:, theirs], wgu_other.at[:, pl.ds(0, HALF)]),
        (wu_hbm.at[:, theirs], wgu_other.at[:, pl.ds(HALF, HALF)]),
        (wd_hbm.at[:, mine], wd_ref.at[feat(w)]),
        (wd_hbm.at[:, theirs], wd_other),
        (og_hbm, og_ref),
    ]
    loads = [pltpu.make_async_copy(a, b, in_sem.at[i]) for i, (a, b) in enumerate(places)]
    for load in loads:
        load.start()

    loads[0].wait()
    loads[1].wait()
    lane = lax.broadcasted_iota(jnp.int32, (EXPERTS, TOK), 0)
    hot = [rt_ref[k:k + 1, :] == lane for k in range(2)]
    named = jnp.where(jnp.logical_or(hot[0], hot[1]), 1.0, 0.0).astype(BF16)
    earlier = jnp.where(
        lax.broadcasted_iota(jnp.int32, (TOK, TOK), 0)
        < lax.broadcasted_iota(jnp.int32, (TOK, TOK), 1), 1.0, 0.0,
    ).astype(BF16)
    before = contract(named, earlier, 1, 0)
    slots = lax.broadcasted_iota(jnp.int32, (ROWS, TOK), 0).astype(F32)
    pick, slot_gate = 0.0, 0.0
    for k in range(2):
        slot = jnp.sum(jnp.where(hot[k], before, 0.0), axis=0, keepdims=True)
        pos = rt_ref[k:k + 1, :].astype(F32) * float(CAP) + slot
        chosen = pos == slots
        pick = pick + jnp.where(chosen, 1.0, 0.0)
        slot_gate = slot_gate + jnp.where(chosen, gp_ref[k:k + 1, :], 0.0)
    slot_gate = jnp.sum(slot_gate, axis=1, keepdims=True)
    pick_ref[...] = pick.astype(BF16)
    loads[2].wait()

    def pick_x(j, carry):
        cols = pl.ds(pl.multiple_of(j * 512, 512), 512)
        send_x[:, cols] = contract(pick_ref[...], tok_ref[:, cols], 1, 0).astype(BF16)
        return carry

    lax.fori_loop(0, 4, pick_x, 0)
    for load in loads[3:9]:
        load.wait()
    pl.semaphore_wait(barrier, len(peers))

    swaps = [
        remote(wgu_other, wgu_ref.at[feat(w)], wo_ssem.at[0], wo_rsem.at[0], partner),
        remote(wd_other, wd_ref.at[feat(w)], wo_ssem.at[1], wo_rsem.at[1], partner),
    ]
    for swap in swaps:
        swap.start()

    def ag_copy(kind, direction, k):
        d = 0 if direction > 0 else 1
        parity = c if (k % 2 == 0) else other
        if k == 6 and direction < 0:
            parity = other
        blk = lax.rem(z - direction * (k // 2) + 2 * RING, RING) * 2 + parity
        ref = (wgu_ref, wd_ref)[kind].at[feat(blk)]
        i = kind * 7 + k
        return remote(ref, ref, ag_ssem.at[d, i], ag_rsem.at[d, i], zdev(direction, c))

    for kind in range(2):
        for direction in (1, -1):
            ag_copy(kind, direction, 0).start()

    own_rows = pl.ds(pl.multiple_of(e * CAP, CAP), CAP)

    def row_copies(src, dst, ssem, rsem):
        out = []
        for i, (dy, dx) in enumerate(OFFSETS):
            dest = edev(dy, dx)
            out.append(remote(
                src.at[pl.ds(pl.multiple_of(dest * CAP, CAP), CAP)],
                dst.at[erow(c, e)], ssem.at[i], rsem.at[i], (dest, w),
            ))
        return out

    x_sends = row_copies(send_x, x_ref, xs_sem, xr_sem)
    for copy in x_sends:
        copy.start()
    x_ref[erow(c, e), :] = send_x[own_rows, :]

    loads[9].wait()

    def pick_g(j, carry):
        cols = pl.ds(pl.multiple_of(j * 512, 512), 512)
        got = contract(pick_ref[...], og_ref[:, cols], 1, 0)
        send_g[:, cols] = (got * slot_gate).astype(BF16)
        return carry

    lax.fori_loop(0, 4, pick_g, 0)
    g_sends = row_copies(send_g, g_ref, gs_sem, gr_sem)
    for copy in g_sends:
        copy.start()
    g_ref[erow(c, e), :] = send_g[own_rows, :]
    for kind in range(2):
        swaps[kind].wait()
        for direction in (1, -1):
            ag_copy(kind, direction, 1).start()

    def forward(buf, ssem, rsem, i, src):
        return remote(buf.at[erow(c, src)], buf.at[erow(c, src)], ssem.at[i], rsem.at[i], partner)

    def pass_on(buf, sends, ssem, rsem, lo, hi):
        for i in range(lo, hi):
            dy, dx = OFFSETS[i]
            sends[i].wait_recv()
            forward(buf, ssem, rsem, i, edev(-dy, -dx)).start()

    def pass_x(lo, hi):
        pass_on(x_ref, x_sends, xfs_sem, xfr_sem, lo, hi)

    def pass_g(lo, hi):
        pass_on(g_ref, g_sends, gfs_sem, gfr_sem, lo, hi)

    def arrived(buf, ssem, rsem):
        for i, (dy, dx) in enumerate(OFFSETS + [(0, 0)]):
            forward(buf, ssem, rsem, i, edev(-dy, -dx)).wait_recv()

    def ag_arrive(kind, k):
        for direction in (1, -1):
            ag_copy(kind, direction, k).wait_recv()
            if direction < 0 and k == 5:
                ag_copy(kind, direction, 6).start()
            elif k + 2 <= 6 and not (direction < 0 and k == 4):
                ag_copy(kind, direction, k + 2).start()

    def add_block(blk, start):
        feats = pl.ds(pl.multiple_of(lax.rem(blk, RING) * 256, 256), 256)

        def tile(t, carry):
            rows = pl.ds(pl.multiple_of(t * 256, 256), 256)
            got = contract(x_ref[rows, feats], wgu_ref[feats, :], 1, 0)
            pre_ref[rows, :] = got if start else pre_ref[rows, :] + got
            return carry

        lax.fori_loop(0, 4, tile, 0)

    def add_more(t, carry):
        add_block(z + RING - 3 + t, False)
        return carry

    def hidden(t, carry):
        rows = pl.ds(pl.multiple_of(t * 32, 32), 32)
        gate_pre = pre_ref[rows, :HALF]
        active = gate_pre * jax.nn.sigmoid(gate_pre)
        hid_ref[rows, :] = (active * pre_ref[rows, HALF:]).astype(BF16)
        return carry

    for k in range(5):
        ag_arrive(0, k)
        ag_arrive(1, k)
        if k == 0:
            forward(x_ref, xfs_sem, xfr_sem, 15, e).start()
            forward(g_ref, gfs_sem, gfr_sem, 15, e).start()
        if k == 3:
            pass_x(0, 8)
        if k == 4:
            pass_x(8, 15)
    ag_arrive(0, 5)
    arrived(x_ref, xfs_sem, xfr_sem)
    add_block(z, True)
    lax.fori_loop(0, 3, add_more, 0)
    ag_arrive(1, 5)
    lax.fori_loop(4, 7, add_more, 0)
    pass_g(0, 6)
    ag_arrive(0, 6)
    add_block(z + 4, False)
    lax.fori_loop(0, 2 * ROWS // 32, hidden, 0)
    ag_arrive(1, 6)
    pass_g(6, 15)
    arrived(g_ref, gfs_sem, gfr_sem)

    bufs = ((sd_send, sd_recv), (su_send, su_recv))

    def partial(kind, blk):
        cols = feat(blk)
        if kind == 0:
            return contract(g_ref[:, cols], hid_ref[...], 0, 0)
        return contract(x_ref[:, cols], act_ref[...], 0, 0)

    def rs_parity(direction, k):
        even = lax.rem(k, 2) == 0
        return jnp.where(even, c, other) if direction > 0 else jnp.where(even, other, c)

    def rs_copy(kind, direction, k):
        d = 0 if direction > 0 else 1
        send, recv = bufs[kind]
        core = jnp.where(k >= 5, rs_parity(direction, k), c)
        return remote(
            send.at[d, k], recv.at[d, k], rs_ssem.at[d, kind * 7 + k],
            rs_rsem.at[d, kind * 7 + k], zdev(direction, core),
        )

    def rs_step(kind, k, add):
        send, recv = bufs[kind]
        for direction in (1, -1):
            d = 0 if direction > 0 else 1
            dist = 4 - (k + 1) // 2
            blk = lax.rem(z + direction * dist + RING, RING) * 2 + rs_parity(direction, k)
            got = partial(kind, blk)
            if add:
                rs_copy(kind, direction, k - 2).wait_recv()
                got = got + recv[d, k - 2].astype(F32)
            send[d, k] = got.astype(BF16)
            rs_copy(kind, direction, k).start()

    def rs_loop(kind, lo, hi, add):
        def step(k, carry):
            rs_step(kind, k, add)
            return carry

        lax.fori_loop(lo, hi, step, 0)

    rs_loop(0, 0, 2, False)

    def second(t, carry):
        rows = pl.ds(pl.multiple_of(t * 512, 512), 512)
        hg_ref[rows, :] = contract(g_ref[rows, :], wd_ref[...], 1, 0)
        return carry

    lax.fori_loop(0, 2, second, 0)

    def swish(t, carry):
        rows = pl.ds(pl.multiple_of(t * 32, 32), 32)
        gate_pre = pre_ref[rows, :HALF]
        up_pre = pre_ref[rows, HALF:]
        hidden_grad = hg_ref[rows, :]
        squash = jax.nn.sigmoid(gate_pre)
        act_ref[rows, :HALF] = (
            hidden_grad * up_pre * squash * (1.0 + gate_pre * (1.0 - squash))
        ).astype(BF16)
        act_ref[rows, HALF:] = (hidden_grad * (gate_pre * squash)).astype(BF16)
        return carry

    lax.fori_loop(0, 2 * ROWS // 32, swish, 0)
    rs_loop(1, 0, 2, False)

    def input_part(core, j):
        rows = pl.ds(pl.multiple_of(core * ROWS, ROWS), ROWS)
        cols = pl.ds(pl.multiple_of(j * 256, 256), 256)
        return contract(act_ref[rows, :], wgu_ref[cols, :], 1, 1), cols

    def for_other(j, carry):
        got, cols = input_part(other, j)
        ig_send[:, cols] = got.astype(BF16)
        return carry

    lax.fori_loop(0, 8, for_other, 0)
    ig_copy = remote(ig_send, ig_recv, ig_sem.at[0], ig_sem.at[1], partner)
    ig_copy.start()
    rs_loop(0, 2, 4, True)

    def for_mine(j, carry):
        got, cols = input_part(c, j)
        ig_own[:, cols] = got
        return carry

    lax.fori_loop(0, 8, for_mine, 0)
    ig_copy.wait_recv()

    def join(t, carry):
        rows = pl.ds(pl.multiple_of(t * CAP, CAP), CAP)
        rg_ref[rows, :] = (ig_own[rows, :] + ig_recv[rows, :].astype(F32)).astype(BF16)
        return carry

    lax.fori_loop(0, EXPERTS, join, 0)
    returns = []
    for i, (dy, dx) in enumerate(OFFSETS):
        dest = edev(dy, dx)
        returns.append(remote(
            rg_ref.at[pl.ds(pl.multiple_of(dest * CAP, CAP), CAP)],
            ret_ref.at[own_rows], ret_ssem.at[i], ret_rsem.at[i], (dest, w),
        ))
    for copy in returns:
        copy.start()
    ret_ref[own_rows, :] = rg_ref[own_rows, :]

    def rs_rest(k, carry):
        rs_step(1, k, True)

        @pl.when(k <= 4)
        def _():
            rs_step(0, k + 2, True)

        return carry

    lax.fori_loop(2, 4, rs_rest, 0)

    fin_send[:, :F] = partial(1, z * 2 + other).astype(BF16)
    fin_send[:, F:] = partial(0, z * 2 + other).astype(BF16)
    fin = remote(fin_send, fin_recv, fin_sem.at[0], fin_sem.at[1], partner)
    fin.start()
    lax.fori_loop(4, 7, rs_rest, 0)
    own_ref[:, :F] = partial(1, w)
    own_ref[:, F:] = partial(0, w)

    for copy in returns:
        copy.wait_recv()

    def combine(j, carry):
        cols = pl.ds(pl.multiple_of(j * 512, 512), 512)
        gi_ref[:, cols] = contract(pick_ref[...], ret_ref[:, cols], 0, 0).astype(BF16)
        return carry

    lax.fori_loop(0, 4, combine, 0)
    fin.wait_recv()

    for kind in range(2):
        recv = bufs[kind][1]
        for direction in (1, -1):
            for k in (5, 6):
                rs_copy(kind, direction, k).wait_recv()
        outs = ((gd_ref, F),) if kind == 0 else ((gg_ref, 0), (gu_ref, HALF))
        for i, (out, lo) in enumerate(outs):
            part = slice(i * HALF, (i + 1) * HALF)
            out[:, mine] = (
                own_ref[:, lo:lo + HALF]
                + recv[0, 6, :, part].astype(F32) + recv[1, 5, :, part].astype(F32)
            )
            out[:, theirs] = (
                fin_recv[:, lo:lo + HALF].astype(F32)
                + recv[0, 5, :, part].astype(F32) + recv[1, 6, :, part].astype(F32)
            )

    for copy in x_sends + g_sends + returns:
        copy.wait_send()
    for i, (dy, dx) in enumerate(OFFSETS + [(0, 0)]):
        src = edev(-dy, -dx)
        forward(x_ref, xfs_sem, xfr_sem, i, src).wait_send()
        forward(g_ref, gfs_sem, gfr_sem, i, src).wait_send()
    for direction in (1, -1):
        for k in range(7):
            for kind in range(2):
                ag_copy(kind, direction, k).wait_send()
                rs_copy(kind, direction, k).wait_send()
    ig_copy.wait_send()
    fin.wait_send()


def store(*refs):
    n = len(refs) // 2
    sem = refs[-1]
    copies = [pltpu.make_async_copy(refs[i], refs[n + i], sem.at[i]) for i in range(n)]
    for copy in copies:
        copy.start()
    for copy in copies:
        copy.wait()


def on_device(tokens, out_grad, routes, gate_prob, w_gate, w_up, w_down):
    flat = [a.reshape(BLK, F) for a in (w_gate, w_up, w_down)]
    dma = pltpu.SemaphoreType.DMA
    vmem = pl.BlockSpec(memory_space=pltpu.VMEM)
    anyw = pl.BlockSpec(memory_space=pl.ANY)
    shapes = [((TOK, D), BF16)] + [((BLK, F), F32)] * 3
    outs = pl.pallas_call(
        kernel,
        name="moe_back",
        out_shape=tuple(pltpu.VMEM(s, t) for s, t in shapes),
        in_specs=[anyw] * 7,
        out_specs=(vmem,) * 4,
        scratch_shapes=[
            pltpu.VMEM((TOK, D), BF16),
            pltpu.VMEM((TOK, D), BF16),
            pltpu.VMEM((2, TOK), jnp.int32),
            pltpu.VMEM((2, TOK), F32),
            pltpu.VMEM((ROWS, D), BF16),
            pltpu.VMEM((ROWS, D), BF16),
            pltpu.VMEM((2 * ROWS, D), BF16),
            pltpu.VMEM((2 * ROWS, D), BF16),
            pltpu.VMEM((D, F), BF16),
            pltpu.VMEM((D, HALF), BF16),
            pltpu.VMEM((BLK, F), BF16),
            pltpu.VMEM((BLK, HALF), BF16),
            pltpu.VMEM((ROWS, TOK), BF16),
            pltpu.VMEM((2 * ROWS, F), F32),
            pltpu.VMEM((2 * ROWS, HALF), F32),
            pltpu.VMEM((2 * ROWS, F), BF16),
            pltpu.VMEM((2 * ROWS, HALF), BF16),
            pltpu.VMEM((2, 7, BLK, HALF), BF16),
            pltpu.VMEM((2, 7, BLK, HALF), BF16),
            pltpu.VMEM((2, 7, BLK, F), BF16),
            pltpu.VMEM((2, 7, BLK, F), BF16),
            pltpu.VMEM((BLK, TRIP), BF16),
            pltpu.VMEM((BLK, TRIP), BF16),
            pltpu.VMEM((BLK, TRIP), F32),
            pltpu.VMEM((ROWS, D), BF16),
            pltpu.VMEM((ROWS, D), BF16),
            pltpu.VMEM((ROWS, D), F32),
            pltpu.VMEM((ROWS, D), BF16),
            pltpu.VMEM((ROWS, D), BF16),
            dma((10,)),
            dma((15,)), dma((15,)), dma((15,)), dma((15,)),
            dma((16,)), dma((16,)), dma((16,)), dma((16,)),
            dma((2,)), dma((2,)), dma((2, 14)), dma((2, 14)), dma((2, 14)), dma((2, 14)),
            dma((2,)), dma((2,)), dma((15,)), dma((15,)),
        ],
        compiler_params=pltpu.CompilerParams(
            collective_id=0, has_side_effects=True, vmem_limit_bytes=56 << 20,
        ),
    )(tokens, out_grad, routes.T, gate_prob.T, *flat)
    outs = pl.pallas_call(
        store,
        name="store",
        out_shape=tuple(jax.ShapeDtypeStruct(s, t) for s, t in shapes),
        in_specs=[vmem] * 4,
        out_specs=(anyw,) * 4,
        scratch_shapes=[dma((4,))],
        compiler_params=pltpu.CompilerParams(vmem_limit_bytes=4 << 20),
    )(*outs)
    return (outs[0],) + tuple(o[None] for o in outs[1:])


def solution(mesh):
    rows = P(("expert", "wide"), None)
    weight = P("expert", "wide", None)
    return jax.shard_map(
        on_device,
        mesh=mesh,
        in_specs=(rows,) * 4 + (weight,) * 3,
        out_specs=(rows,) + (weight,) * 3,
        check_vma=False,
    )
```

time: 132 us -> 115 us (0.87)
  the two profiles are of different devices: /device:TPU:33 before, /device:TPU:17 now
where the time goes in v2:
time: 115 us
  Pallas kernels  114 us (99%)
    pallas_call x1, Pallas kernels, on_device(): pl.pallas_call(kernel, name='moe_back', out_shape=tuple((pltpu.VMEM(s, t)...  113 us

profile of v2, /device:TPU:17, one launch (start us, length us, event | category | flops | bytes accessed | tf_op | source)
XLA Modules:
  0.0 114.7 jit_solution(4012421852116301235)
XLA Ops:
  0.6 112.8 %moe_back.1 = (bf16[128,2048]{1,0:T(8,128)(2,1)S(1)}, f32[128,768]{1,0:T(8,128)S(1)}, f32[128,768]{1,0:T(8,128)S(1)}, f32[128,768]{1,0:T(8,128)S(1)}) custom-call(bf16[128,2048]{1,0:T(8,128)(2,1)} %tok_hbm.1, bf16[128,2048]{1,0:T(8,128)(2,1)} %og_hbm.1, s32[2,128]{1,0:T(2,128)} %bitcast.11, f32[2,128]{1,0:T(2,128)} %bitcast.12, bf16[128,768]{1,0:T(8,128)(2,1)} %bitcast.8, ...), custom_call_target="tpu_custom_call" | custom-call | tf_op jit(solution)/shard_map/moe_back/pallas_call | solution.py:437
  113.4 1.2 %store.1 = (bf16[128,2048]{1,0:T(8,128)(2,1)}, f32[128,768]{1,0:T(8,128)}, f32[128,768]{1,0:T(8,128)}, f32[128,768]{1,0:T(8,128)}) custom-call(bf16[128,2048]{1,0:T(8,128)(2,1)S(1)} %get-tuple-element.12.refs_0_, f32[128,768]{1,0:T(8,128)S(1)} %get-tuple-element.13.refs_1_, f32[128,768]{1,0:T(8,128)S(1)} %get-tuple-element.14.refs_2_, ...), custom_call_target="tpu_custom_call" | custom-call | tf_op jit(solution)/shard_map/store/pallas_call | solution.py:483

commit v3 on v2

--- a/solution.py
+++ b/solution.py
@@ -249,7 +249,6 @@
     lax.fori_loop(0, 2 * ROWS // 32, hidden, 0)
     ag_arrive(1, 6)
     pass_g(6, 15)
-    arrived(g_ref, gfs_sem, gfr_sem)
 
     bufs = ((sd_send, sd_recv), (su_send, su_recv))
 
@@ -292,7 +291,19 @@
 
         lax.fori_loop(lo, hi, step, 0)
 
-    rs_loop(0, 0, 2, False)
+    def first_part(direction, core):
+        rows = pl.ds(pl.multiple_of(core * ROWS, ROWS), ROWS)
+        blk = lax.rem(z + 4, RING) * 2 + (c if direction > 0 else other)
+        return contract(g_ref[rows, feat(blk)], hid_ref[rows, :], 0, 0)
+
+    for d, direction in enumerate((1, -1)):
+        own_ref[:, d * HALF:(d + 1) * HALF] = first_part(direction, c)
+    arrived(g_ref, gfs_sem, gfr_sem)
+    for d, direction in enumerate((1, -1)):
+        got = own_ref[:, d * HALF:(d + 1) * HALF] + first_part(direction, other)
+        sd_send[d, 0] = got.astype(BF16)
+        rs_copy(0, direction, 0).start()
+    rs_loop(0, 1, 2, False)
 
     def second(t, carry):
         rows = pl.ds(pl.multiple_of(t * 512, 512), 512)

time: 115 us -> 115 us (level)
  no operation moved by 1% of the time
where the time goes in v3:
time: 115 us; the launch traced here: 114 us
  Pallas kernels  114 us (99%)
    pallas_call x1, Pallas kernels, on_device(): pl.pallas_call(kernel, name='moe_back', out_shape=tuple((pltpu.VMEM(s, t)...  113 us

profile of v3, /device:TPU:17, one launch (start us, length us, event | category | flops | bytes accessed | tf_op | source)
XLA Modules:
  0.0 114.5 jit_solution(484223787484652470)
XLA Ops:
  0.6 112.6 %moe_back.1 = (bf16[128,2048]{1,0:T(8,128)(2,1)S(1)}, f32[128,768]{1,0:T(8,128)S(1)}, f32[128,768]{1,0:T(8,128)S(1)}, f32[128,768]{1,0:T(8,128)S(1)}) custom-call(bf16[128,2048]{1,0:T(8,128)(2,1)} %tok_hbm.1, bf16[128,2048]{1,0:T(8,128)(2,1)} %og_hbm.1, s32[2,128]{1,0:T(2,128)} %bitcast.11, f32[2,128]{1,0:T(2,128)} %bitcast.12, bf16[128,768]{1,0:T(8,128)(2,1)} %bitcast.8, ...), custom_call_target="tpu_custom_call" | custom-call | tf_op jit(solution)/shard_map/moe_back/pallas_call | solution.py:448
  113.3 1.2 %store.1 = (bf16[128,2048]{1,0:T(8,128)(2,1)}, f32[128,768]{1,0:T(8,128)}, f32[128,768]{1,0:T(8,128)}, f32[128,768]{1,0:T(8,128)}) custom-call(bf16[128,2048]{1,0:T(8,128)(2,1)S(1)} %get-tuple-element.12.refs_0_, f32[128,768]{1,0:T(8,128)S(1)} %get-tuple-element.13.refs_1_, f32[128,768]{1,0:T(8,128)S(1)} %get-tuple-element.14.refs_2_, ...), custom_call_target="tpu_custom_call" | custom-call | tf_op jit(solution)/shard_map/store/pallas_call | solution.py:494
